TPU v7x, 128 devices: a whole 4x4x4 slice. The times are simulated.
128 devices in a mesh: gx: 16 (over z, y_lo, core), gy: 8 (over y_hi, x).
Axes of the slice: x: 4, y: 4 (y_hi: 2, y_lo: 2; y = y_hi * 2 + y_lo), z: 4, core: 2. Of those that a mesh axis runs over, the one named last changes fastest.
Arguments:
- points: bfloat16 [64, 262144], P(None, ('gx', 'gy')), may hold values from -6 to 6
- vectors: bfloat16 [32, 262144], P(None, ('gx', 'gy')), may hold values from -6 to 6
- leaf_pick: int32 [512, 128], P(('gx', 'gy')), may hold values from 0 to 511
- leaf_assign: int32 [512, 512], P(('gx', 'gy')), may hold values from 0 to 127
- device_pick: int32 [128, 128], P(('gx', 'gy')), may hold values from 0 to 511
- device_assign: int32 [128, 512], P(('gx', 'gy')), may hold values from 0 to 127
- node_pick: int32 [16, 7, 128], P('gx'), may hold values from 0 to 255
- node_assign: int32 [16, 7, 256], P('gx'), may hold values from 0 to 127
- far_mask: int32 [16, 16], P('gx'), may hold values from 0 to 1, as said below
- near_lower: int32 [128, 8, 12], P(('gx', 'gy')), may hold values from -1 to 3, as said below
- near_upper: int32 [128, 8, 12], P(('gx', 'gy')), may hold values from 0 to 3, as said below
Outputs:
- potential: float32 [32, 262144], P(None, ('gx', 'gy'))
Inputs may be any that keep to these rules, and one draw needn't show every extreme that they name: near_lower[d, o, j] is a local leaf of device d forming a near pair with local leaf near_upper[d, o, j] of device d + o + 1, or -1 for an empty slot; the slots of one d and o never name the same pair of leaves, and no live slot names a device past the last. `near_upper`: A local leaf of device d + o + 1, read only where near_lower is live. `far_mask`: Symmetric, zero on the diagonal, one where the two group indices differ by exactly 1.
All inputs are finite; a program needn't handle non-finite values.
Results may differ from a plain program's by a relative error of at most 0.0015.
Values may be sent and summed in bfloat16 or wider, within the bound.
A program may use at most 128 MiB of HBM per device.

v0:
```python
import jax
import jax.numpy as jnp
from jax import lax
from jax.experimental import pallas as pl
from jax.experimental.pallas import tpu as pltpu
from jax.sharding import PartitionSpec as P

DIM = 64
COLS = 32
LEAF = 512
SKEL = 128
LPD = 4
BLOCK = LPD * LEAF
SLOTS = 12
NGX = 16
NGY = 8
RING = 4
AUG = 128
CHUNK = SKEL // NGY
STRIP = 128
MESH = pl.DeviceIdType.MESH
BF = jnp.bfloat16
F32 = jnp.float32


def nn(a, b, precision=None):
    return lax.dot_general(
        a, b, (((1,), (0,)), ((), ())), preferred_element_type=F32, precision=precision
    )


def nt(a, b):
    return lax.dot_general(a, b, (((1,), (1,)), ((), ())), preferred_element_type=F32)


def three_parts(row):
    high = row.astype(BF).astype(F32)
    rest = row - high
    middle = rest.astype(BF).astype(F32)
    return high, middle, rest - middle


def tail_rows(points, norm_first):
    wide = points.astype(F32)
    parts = three_parts(jnp.sum(wide * wide, axis=0, keepdims=True) * (-1.0 / 32.0))
    row = lax.broadcasted_iota(jnp.int32, (DIM, points.shape[1]), 0)
    at = 0 if norm_first else 3
    ones_at = 3 - at
    tail = jnp.where((row >= ones_at) & (row < ones_at + 3), 1.0, 0.0)
    for k in range(3):
        tail = jnp.where(row == at + k, parts[k], tail)
    return tail.astype(BF)


def build_upper(points, upper_ref, which):
    for leaf in range(LPD):
        cols = pl.ds(leaf * LEAF, LEAF)
        chunk = points[:, cols]
        upper_ref[which, leaf, 0:DIM, :] = chunk
        upper_ref[which, leaf, DIM:AUG, :] = tail_rows(chunk, False)


def build_lower(points, lower_ref):
    for leaf in range(LPD):
        cols = pl.ds(leaf * LEAF, LEAF)
        chunk = points[:, cols]
        both = jnp.concatenate([chunk * BF(1.0 / 16.0), tail_rows(chunk, True)], axis=0)
        lower_ref[leaf] = both.T


def build_leaves(vectors, leaves_ref):
    for leaf in range(LPD):
        leaves_ref[leaf] = vectors[:, leaf * LEAF : (leaf + 1) * LEAF]


def kernel_tile(lower_ref, upper_ref, which, low, high, out_ref):
    upper = upper_ref[which, high]
    for at in range(0, LEAF, STRIP):
        exponent = nn(lower_ref[low, at : at + STRIP, :], upper)
        out_ref[at : at + STRIP, :] = jnp.exp(exponent).astype(BF)


def fused(
    points_ref,
    vectors_ref,
    leaf_pick_ref,
    leaf_assign_ref,
    device_pick_ref,
    device_assign_ref,
    node_pick_ref,
    node_assign_ref,
    far_mask_ref,
    low_s,
    high_s,
    low_v,
    high_v,
    out_ref,
    got_points,
    got_vectors,
    upper_vectors,
    lower_vectors,
    codes_v,
    codes_s,
    lower,
    upper,
    acc_low,
    acc_up,
    send_terms,
    got_terms,
    tile_a,
    tile_b,
    composed,
    share,
    share_got,
    chunk_sum,
    roots,
    targets,
    part,
    part_got,
    near_send,
    near_recv,
    code_send,
    code_recv,
    code_local,
    pass_send,
    pass_recv,
    back_send,
    back_recv,
    share_send,
    share_recv,
    root_send,
    root_recv,
    target_send,
    target_recv,
    part_send,
    part_recv,
):
    gx = lax.axis_index("gx")
    gy = lax.axis_index("gy")
    flat = gx * NGY + gy
    x = gy % RING
    base = gy - x

    def at_flat(step):
        other = lax.rem(flat + step + NGX * NGY, NGX * NGY)
        return (other // NGY, lax.rem(other, NGY))

    def in_ring(step):
        return (gx, base + lax.rem(x + step, RING))

    def mate_gy(step):
        return (gx, lax.rem(gy + step, NGY))

    def mate_gx(step):
        return (lax.rem(gx + step, NGX), gy)

    barrier = pltpu.get_barrier_semaphore()
    greeted = [mate_gy(s) for s in range(1, NGY)] + [mate_gx(s) for s in range(1, NGX)]
    greeted += [at_flat(4), at_flat(-4), at_flat(8), at_flat(-8)]
    for device in greeted:
        pl.semaphore_signal(barrier, inc=1, device_id=device, device_id_type=MESH)
    pl.semaphore_wait(barrier, len(greeted))

    started = []

    def send(src, dst, send_sem, recv_sem, device):
        copy = pltpu.make_async_remote_copy(
            src_ref=src,
            dst_ref=dst,
            send_sem=send_sem,
            recv_sem=recv_sem,
            device_id=device,
            device_id_type=MESH,
        )
        copy.start()
        started.append(copy)
        return copy

    ring_steps = (1, 3, 2)
    code_copies = []
    for k, step in enumerate(ring_steps):
        to = in_ring(RING - step)
        code_copies.append(
            (
                send(low_v, codes_v.at[k, 0], code_send.at[2 * k], code_recv.at[2 * k], to),
                send(high_v, codes_v.at[k, 1], code_send.at[2 * k + 1], code_recv.at[2 * k + 1], to),
            )
        )
    near = [None] * 5

    def send_block(slot, device):
        vector_dst = got_vectors.at[slot]
        near[slot] = (
            send(points_ref, got_points.at[slot], near_send.at[2 * slot], near_recv.at[2 * slot], device),
            send(vectors_ref, vector_dst, near_send.at[2 * slot + 1], near_recv.at[2 * slot + 1], device),
        )

    send_block(1, at_flat(-8))
    send_block(0, at_flat(-4))
    send_block(2, in_ring(3))
    send_block(3, in_ring(1))

    build_leaves(vectors_ref, upper_vectors.at[0])
    build_leaves(vectors_ref, lower_vectors)
    build_upper(points_ref, upper, 0)
    build_lower(points_ref, lower)
    acc_up[...] = jnp.zeros_like(acc_up)
    acc_low[...] = jnp.zeros_like(acc_low)

    heaps = (3 + gy // 2, 1 + gy // 4, 0)
    sides = (gy % 2, (gy // 2) % 2, gy // 4)
    square = lax.broadcasted_iota(jnp.int32, (SKEL, SKEL), 0)

    def hot(condition):
        return jnp.where(condition, 1.0, 0.0).astype(BF)

    path = None
    for level in range(3):
        row = node_assign_ref[
            heaps[level], :, pl.ds(pl.multiple_of(sides[level] * SKEL, SKEL), SKEL)
        ]
        step = hot(square == row)
        path = step if path is None else nn(step, path).astype(BF)
    tall = lax.broadcasted_iota(jnp.int32, (SKEL, LEAF), 0)
    weights = jnp.zeros((SKEL, COLS), F32)
    for leaf in range(LPD):
        cols = slice(leaf * LEAF, (leaf + 1) * LEAF)
        skel = slice(leaf * SKEL, (leaf + 1) * SKEL)
        to_root = nn(path, hot(square == device_assign_ref[:, skel])).astype(BF)
        whole = nn(to_root, hot(tall == leaf_assign_ref[leaf : leaf + 1, :])).astype(BF)
        composed[:, cols] = whole
        weights += nt(whole, vectors_ref[:, cols])
    leaf_rows = lax.broadcasted_iota(jnp.int32, (LEAF, SKEL), 0)
    node_points = jnp.zeros((DIM, SKEL), F32)
    for leaf in range(LPD):
        cols = slice(leaf * LEAF, (leaf + 1) * LEAF)
        picked = nn(points_ref[:, cols], hot(leaf_rows == leaf_pick_ref[leaf : leaf + 1, :]))
        node_points += nn(picked.astype(BF), hot(square + leaf * SKEL == device_pick_ref[...]))
    for level in range(3):
        picks = node_pick_ref[heaps[level]]
        node_points = nn(node_points.astype(BF), hot(square + sides[level] * SKEL == picks))
    share[:, 0:DIM] = jnp.concatenate([node_points, jnp.zeros((SKEL - DIM, SKEL), F32)], axis=0).T[:, 0:DIM]
    share[:, DIM : DIM + COLS] = weights
    share[:, DIM + COLS :] = jnp.zeros((SKEL, SKEL - DIM - COLS), F32)

    def apply_own(tile_ref, low, high):
        low_at = pl.multiple_of(low * LEAF, LEAF)
        high_at = pl.multiple_of(high * LEAF, LEAF)
        tile = tile_ref[...]
        acc_up[0, :, pl.ds(high_at, LEAF)] += nn(upper_vectors[0, low], tile)
        acc_low[0, :, pl.ds(low_at, LEAF)] += nt(upper_vectors[0, high], tile)

    def own_pair(n):
        low = (n >= 3).astype(jnp.int32) + (n >= 5).astype(jnp.int32)
        high = jnp.where(n < 3, n + 1, jnp.where(n < 5, n - 1, 3))
        return low, high

    kernel_tile(lower, upper, 0, 0, 1, tile_a)

    def own_step(m, carry):
        low0, high0 = own_pair(2 * m)
        low1, high1 = own_pair(2 * m + 1)
        low2, high2 = own_pair(jnp.minimum(2 * m + 2, 5))
        kernel_tile(lower, upper, 0, low1, high1, tile_b)
        apply_own(tile_a, low0, high0)
        kernel_tile(lower, upper, 0, low2, high2, tile_a)
        apply_own(tile_b, low1, high1)
        return carry

    lax.fori_loop(0, 3, own_step, 0)

    def own_diagonal(leaf, carry):
        at = pl.multiple_of(leaf * LEAF, LEAF)
        kernel_tile(lower, upper, 0, leaf, leaf, tile_a)
        acc_up[0, :, pl.ds(at, LEAF)] += nn(upper_vectors[0, leaf], tile_a[...])
        return carry

    lax.fori_loop(0, LPD, own_diagonal, 0)

    share_copies = []
    for s in range(1, NGY):
        to = mate_gy(s)
        rows = pl.ds(pl.multiple_of(to[1] * CHUNK, CHUNK), CHUNK)
        share_copies.append(
            send(share.at[rows, :], share_got.at[s - 1], share_send.at[s - 1], share_recv.at[s - 1], to)
        )

    for copy in near[0]:
        copy.wait_recv()
    for copy in near[1]:
        copy.wait_recv()
    build_upper(got_points.at[0], upper, 1)
    build_upper(got_points.at[1], upper, 2)
    build_leaves(got_vectors.at[0], upper_vectors.at[1])
    build_leaves(got_vectors.at[1], upper_vectors.at[2])

    def stage(k, step, low_codes, high_codes):
        i = lax.rem(x + step, RING)
        first = RING + x - i - 1
        other = jnp.where(i < x, x - i - 1, 2 * RING + x - i - 1)
        other_upper = jnp.where(i < x, 0, 2)

        def slot(n):
            far_half = n >= SLOTS
            offset = jnp.where(far_half, other, first)
            which = jnp.where(far_half, other_upper, 1)
            at = n - jnp.where(far_half, SLOTS, 0)
            return low_codes[offset, at], high_codes[offset, at], which

        def make(n, tile_ref):
            low, high, which = slot(n)
            kernel_tile(lower, upper, which, jnp.maximum(low, 0), high, tile_ref)

        def apply(n, tile_ref):
            low, high, which = slot(n)
            tile = tile_ref[...]
            to_upper = nn(lower_vectors[jnp.maximum(low, 0)], tile)
            to_lower = nt(upper_vectors[which, high], tile)
            live = low >= 0
            for leaf in range(LPD):
                cols = slice(leaf * LEAF, (leaf + 1) * LEAF)
                acc_up[which, :, cols] += jnp.where(live & (high == leaf), to_upper, 0.0)
                acc_low[k, :, cols] += jnp.where(low == leaf, to_lower, 0.0)

        make(0, tile_a)

        def pair(m, carry):
            make(2 * m + 1, tile_b)
            apply(2 * m, tile_a)
            make(jnp.minimum(2 * m + 2, 2 * SLOTS - 1), tile_a)
            apply(2 * m + 1, tile_b)
            return carry

        lax.fori_loop(0, SLOTS, pair, 0)

    stage(0, 0, low_s, high_s)

    for copy in share_copies:
        copy.wait_recv()
    mine = pl.ds(pl.multiple_of(gy * CHUNK, CHUNK), CHUNK)
    total = share[mine, :]
    for s in range(NGY - 1):
        total += share_got[s]
    chunk_sum[...] = total
    roots[0] = total
    targets[mine, :] = total

    for slot in (2, 3):
        for copy in near[slot]:
            copy.wait_recv()
    half = BLOCK // 2
    forwards = []
    for part_index, (slot, step, start) in enumerate(((2, 3, 0), (3, 1, half))):
        cols = pl.ds(start, half)
        to = in_ring(step)
        forwards.append(
            send(
                got_points.at[slot, :, cols],
                got_points.at[4, :, cols],
                pass_send.at[2 * part_index],
                pass_recv.at[2 * part_index],
                to,
            )
        )
        forwards.append(
            send(
                got_vectors.at[slot, :, cols],
                got_vectors.at[4, :, cols],
                pass_send.at[2 * part_index + 1],
                pass_recv.at[2 * part_index + 1],
                to,
            )
        )
    root_copies = []
    for s in range(1, NGX):
        root_copies.append(
            send(chunk_sum, roots.at[NGX - s], root_send.at[s - 1], root_recv.at[s - 1], mate_gx(s))
        )
    target_copies = []
    for s in range(1, NGY):
        target_copies.append(
            send(chunk_sum, targets.at[mine, :], target_send.at[s - 1], target_recv.at[s - 1], mate_gy(s))
        )
    for pair in code_copies:
        for copy in pair:
            copy.wait_recv()
    local = []
    for k in range(3):
        for h in range(2):
            copy = pltpu.make_async_copy(codes_v.at[k, h], codes_s.at[k, h], code_local.at[2 * k + h])
            copy.start()
            local.append(copy)
    for copy in local:
        copy.wait()

    def give_back(slot, terms, device):
        send_terms[slot] = terms.astype(BF)
        return send(send_terms.at[slot], got_terms.at[slot], back_send.at[slot], back_recv.at[slot], device)

    returned = []

    def ring_stage(k, step, slot):
        build_lower(got_points.at[slot], lower)
        build_leaves(got_vectors.at[slot], lower_vectors)
        stage(
            k,
            step,
            codes_s.at[slot - 2, 0],
            codes_s.at[slot - 2, 1],
        )

    ring_stage(1, 1, 2)
    returned.append(give_back(2, acc_low[1], in_ring(1)))

    for copy in root_copies:
        copy.wait_recv()
    for copy in target_copies:
        copy.wait_recv()
    sources = roots[...].reshape(NGX * CHUNK, SKEL)
    goals = targets[...]
    source_points = sources[:, 0:DIM]
    goal_points = goals.T[0:DIM, :]
    source_norm = jnp.sum(source_points * source_points, axis=1, keepdims=True)
    goal_norm = jnp.sum(goal_points * goal_points, axis=0, keepdims=True)
    products = nn(source_points.astype(BF), goal_points.astype(BF))
    root_kernel = jnp.exp((-2.0 / DIM) * (source_norm + goal_norm - 2.0 * products))
    source_group = lax.broadcasted_iota(jnp.int32, (NGX * CHUNK, NGX), 0) // CHUNK
    group_id = lax.rem(source_group + gx, NGX)
    listed = lax.broadcasted_iota(jnp.int32, (NGX * CHUNK, NGX), 1) == group_id
    flags = jnp.sum(jnp.where(listed, far_mask_ref[...].astype(F32), 0.0), axis=1, keepdims=True)
    flagged = (sources * flags).T[DIM : DIM + COLS, :]
    part[...] = nn(flagged, root_kernel, lax.Precision.HIGHEST)
    part_copies = []
    for s in range(1, NGY):
        part_copies.append(
            send(part, part_got.at[s - 1], part_send.at[s - 1], part_recv.at[s - 1], mate_gy(s))
        )

    ring_stage(2, 3, 3)
    returned.append(give_back(3, acc_low[2], in_ring(3)))
    for copy in forwards:
        copy.wait_recv()
    ring_stage(3, 2, 4)
    returned.append(give_back(4, acc_low[3], in_ring(2)))
    returned.append(give_back(0, acc_up[1], at_flat(4)))
    returned.append(give_back(1, acc_up[2], at_flat(8)))

    for copy in part_copies:
        copy.wait_recv()
    potential = part[...]
    for s in range(NGY - 1):
        potential += part_got[s]
    parts = [p.astype(BF) for p in three_parts(potential)]
    for leaf in range(LPD):
        cols = slice(leaf * LEAF, (leaf + 1) * LEAF)
        terms = acc_up[0, :, cols] + acc_low[0, :, cols]
        for p in parts:
            terms += nn(p, composed[:, cols])
        acc_up[0, :, cols] = terms

    for copy in returned:
        copy.wait_recv()
    total_terms = acc_up[0]
    for slot in range(5):
        total_terms += got_terms[slot].astype(F32)
    out_ref[...] = total_terms
    for copy in started:
        copy.wait_send()


def on_device(
    points,
    vectors,
    leaf_pick,
    leaf_assign,
    device_pick,
    device_assign,
    node_pick,
    node_assign,
    far_mask,
    near_lower,
    near_upper,
):
    vmem = pl.BlockSpec(memory_space=pltpu.VMEM)
    smem = pl.BlockSpec(memory_space=pltpu.SMEM)
    dma = pltpu.SemaphoreType.DMA
    low, high = near_lower[0], near_upper[0]
    reach = low.shape[0]
    return pl.pallas_call(
        fused,
        out_shape=jax.ShapeDtypeStruct((COLS, BLOCK), F32),
        in_specs=[vmem] * 9 + [smem] * 2 + [vmem] * 2,
        out_specs=vmem,
        scratch_shapes=[
            pltpu.VMEM((5, DIM, BLOCK), BF),
            pltpu.VMEM((5, COLS, BLOCK), BF),
            pltpu.VMEM((3, LPD, COLS, LEAF), BF),
            pltpu.VMEM((LPD, COLS, LEAF), BF),
            pltpu.VMEM((3, 2, reach, SLOTS), jnp.int32),
            pltpu.SMEM((3, 2, reach, SLOTS), jnp.int32),
            pltpu.VMEM((LPD, LEAF, AUG), BF),
            pltpu.VMEM((3, LPD, AUG, LEAF), BF),
            pltpu.VMEM((RING, COLS, BLOCK), F32),
            pltpu.VMEM((3, COLS, BLOCK), F32),
            pltpu.VMEM((5, COLS, BLOCK), BF),
            pltpu.VMEM((5, COLS, BLOCK), BF),
            pltpu.VMEM((LEAF, LEAF), BF),
            pltpu.VMEM((LEAF, LEAF), BF),
            pltpu.VMEM((SKEL, BLOCK), BF),
            pltpu.VMEM((SKEL, SKEL), F32),
            pltpu.VMEM((NGY - 1, CHUNK, SKEL), F32),
            pltpu.VMEM((CHUNK, SKEL), F32),
            pltpu.VMEM((NGX, CHUNK, SKEL), F32),
            pltpu.VMEM((SKEL, SKEL), F32),
            pltpu.VMEM((COLS, SKEL), F32),
            pltpu.VMEM((NGY - 1, COLS, SKEL), F32),
            dma((10,)),
            dma((10,)),
            dma((6,)),
            dma((6,)),
            dma((6,)),
            dma((4,)),
            dma((4,)),
            dma((5,)),
            dma((5,)),
            dma((NGY - 1,)),
            dma((NGY - 1,)),
            dma((NGX - 1,)),
            dma((NGX - 1,)),
            dma((NGY - 1,)),
            dma((NGY - 1,)),
            dma((NGY - 1,)),
            dma((NGY - 1,)),
        ],
        compiler_params=pltpu.CompilerParams(
            collective_id=0, has_side_effects=True, vmem_limit_bytes=56 * 2**20
        ),
        name="treecode",
    )(
        points,
        vectors,
        leaf_pick,
        leaf_assign,
        device_pick,
        device_assign,
        node_pick[0][:, None, :],
        node_assign[0][:, None, :],
        far_mask,
        low,
        high,
        low,
        high,
    )


def solution(mesh):
    placed = (
        P(None, ("gx", "gy")),
        P(None, ("gx", "gy")),
        P(("gx", "gy"), None),
        P(("gx", "gy"), None),
        P(("gx", "gy"), None),
        P(("gx", "gy"), None),
        P("gx", None, None),
        P("gx", None, None),
        P("gx", None),
        P(("gx", "gy"), None, None),
        P(("gx", "gy"), None, None),
    )
    return jax.shard_map(
        on_device, mesh=mesh, in_specs=placed, out_specs=P(None, ("gx", "gy")), check_vma=False
    )
```

profile of v0, /device:TPU:0, one launch (start us, length us, event | category | flops | bytes accessed | tf_op | source)
XLA Modules:
  0.0 79.7 jit_solution(10252688195221897647)
XLA Ops:
  0.0 78.1 %treecode.1 = f32[32,2048]{1,0:T(8,128)} custom-call(bf16[64,2048]{1,0:T(8,128)(2,1)} %points_ref.1, bf16[32,2048]{1,0:T(8,128)(2,1)} %vectors_ref.1, s32[4,128]{1,0:T(4,128)} %leaf_pick_ref.1, s32[4,512]{1,0:T(4,128)} %leaf_assign_ref.1, s32[1,128]{1,0:T(1,128)} %device_pick_ref.1, s32[1,512]{1,0:T(1,128)} %device_assign_ref.1, s32[7,1,128]{2,1,0:T(1,128)} %bitcast.9, ...), custom_call_target="tpu_custom_call" | custom-call | tf_op jit(solution)/shard_map/treecode/pallas_call | solution.py:489
  78.1 1.7 %copy.13 = f32[32,2048]{1,0:T(8,128)} copy(f32[32,2048]{1,0:T(8,128)} %treecode.1) | data formatting | bytes 524288
where the time goes:
time: 79.9 us; the launch traced here: 79.7 us
  Pallas kernels  78.1 us (98%)
  local copies, waits for them, and re-layouts  1.67 us (2%)
    pallas_call x1, Pallas kernels, on_device(): pl.pallas_call(fused, out_shape=jax.ShapeDtypeStruct((COLS, BLOCK), F32),...  78.1 us
    unnamed x1, local copies, waits for them, and re-layouts  1.67 us

commit v1 on v0

--- a/solution.py
+++ b/solution.py
@@ -17,7 +17,9 @@
 RING = 4
 AUG = 128
 CHUNK = SKEL // NGY
-STRIP = 128
+STAGES = (0, 1, 2, 3)
+HALF = LEAF // 2
+UNROLL = 3
 MESH = pl.DeviceIdType.MESH
 BF = jnp.bfloat16
 F32 = jnp.float32
@@ -73,16 +75,13 @@
         leaves_ref[leaf] = vectors[:, leaf * LEAF : (leaf + 1) * LEAF]
 
 
-def kernel_tile(lower_ref, upper_ref, which, low, high, out_ref):
-    upper = upper_ref[which, high]
-    for at in range(0, LEAF, STRIP):
-        exponent = nn(lower_ref[low, at : at + STRIP, :], upper)
-        out_ref[at : at + STRIP, :] = jnp.exp(exponent).astype(BF)
+def tile_rows(lower_rows, upper, out_ref, at):
+    out_ref[at : at + HALF, :] = jnp.exp(nn(lower_rows, upper)).astype(BF)
 
 
 def fused(
-    points_ref,
-    vectors_ref,
+    points_hbm,
+    vectors_hbm,
     leaf_pick_ref,
     leaf_assign_ref,
     device_pick_ref,
@@ -95,6 +94,8 @@
     low_v,
     high_v,
     out_ref,
+    points_ref,
+    vectors_ref,
     got_points,
     got_vectors,
     upper_vectors,
@@ -122,6 +123,7 @@
     code_send,
     code_recv,
     code_local,
+    own_sem,
     pass_send,
     pass_recv,
     back_send,
@@ -159,6 +161,20 @@
     greeted += [at_flat(4), at_flat(-4), at_flat(8), at_flat(-8)]
     for device in greeted:
         pl.semaphore_signal(barrier, inc=1, device_id=device, device_id_type=MESH)
+    own_copies = [
+        pltpu.make_async_copy(points_hbm, points_ref, own_sem.at[0]),
+        pltpu.make_async_copy(vectors_hbm, vectors_ref, own_sem.at[1]),
+    ]
+    for copy in own_copies:
+        copy.start()
+    acc_up[...] = jnp.zeros_like(acc_up)
+    acc_low[...] = jnp.zeros_like(acc_low)
+    for copy in own_copies:
+        copy.wait()
+    build_leaves(vectors_ref, upper_vectors.at[0])
+    build_leaves(vectors_ref, lower_vectors.at[0])
+    build_upper(points_ref, upper, 0)
+    build_lower(points_ref, lower.at[0])
     pl.semaphore_wait(barrier, len(greeted))
 
     started = []
@@ -176,9 +192,8 @@
         started.append(copy)
         return copy
 
-    ring_steps = (1, 3, 2)
     code_copies = []
-    for k, step in enumerate(ring_steps):
+    for k, step in enumerate(STAGES[1:]):
         to = in_ring(RING - step)
         code_copies.append(
             (
@@ -199,13 +214,6 @@
     send_block(0, at_flat(-4))
     send_block(2, in_ring(3))
     send_block(3, in_ring(1))
-
-    build_leaves(vectors_ref, upper_vectors.at[0])
-    build_leaves(vectors_ref, lower_vectors)
-    build_upper(points_ref, upper, 0)
-    build_lower(points_ref, lower)
-    acc_up[...] = jnp.zeros_like(acc_up)
-    acc_low[...] = jnp.zeros_like(acc_low)
 
     heaps = (3 + gy // 2, 1 + gy // 4, 0)
     sides = (gy % 2, (gy // 2) % 2, gy // 4)
@@ -243,40 +251,6 @@
     share[:, DIM : DIM + COLS] = weights
     share[:, DIM + COLS :] = jnp.zeros((SKEL, SKEL - DIM - COLS), F32)
 
-    def apply_own(tile_ref, low, high):
-        low_at = pl.multiple_of(low * LEAF, LEAF)
-        high_at = pl.multiple_of(high * LEAF, LEAF)
-        tile = tile_ref[...]
-        acc_up[0, :, pl.ds(high_at, LEAF)] += nn(upper_vectors[0, low], tile)
-        acc_low[0, :, pl.ds(low_at, LEAF)] += nt(upper_vectors[0, high], tile)
-
-    def own_pair(n):
-        low = (n >= 3).astype(jnp.int32) + (n >= 5).astype(jnp.int32)
-        high = jnp.where(n < 3, n + 1, jnp.where(n < 5, n - 1, 3))
-        return low, high
-
-    kernel_tile(lower, upper, 0, 0, 1, tile_a)
-
-    def own_step(m, carry):
-        low0, high0 = own_pair(2 * m)
-        low1, high1 = own_pair(2 * m + 1)
-        low2, high2 = own_pair(jnp.minimum(2 * m + 2, 5))
-        kernel_tile(lower, upper, 0, low1, high1, tile_b)
-        apply_own(tile_a, low0, high0)
-        kernel_tile(lower, upper, 0, low2, high2, tile_a)
-        apply_own(tile_b, low1, high1)
-        return carry
-
-    lax.fori_loop(0, 3, own_step, 0)
-
-    def own_diagonal(leaf, carry):
-        at = pl.multiple_of(leaf * LEAF, LEAF)
-        kernel_tile(lower, upper, 0, leaf, leaf, tile_a)
-        acc_up[0, :, pl.ds(at, LEAF)] += nn(upper_vectors[0, leaf], tile_a[...])
-        return carry
-
-    lax.fori_loop(0, LPD, own_diagonal, 0)
-
     share_copies = []
     for s in range(1, NGY):
         to = mate_gy(s)
@@ -284,103 +258,146 @@
         share_copies.append(
             send(share.at[rows, :], share_got.at[s - 1], share_send.at[s - 1], share_recv.at[s - 1], to)
         )
-
-    for copy in near[0]:
-        copy.wait_recv()
-    for copy in near[1]:
-        copy.wait_recv()
+    mine = pl.ds(pl.multiple_of(gy * CHUNK, CHUNK), CHUNK)
+    half = BLOCK // 2
+
+    def masked(ref, index, codes, base_col, terms):
+        for leaf in range(LPD):
+            cols = slice(leaf * LEAF + base_col, leaf * LEAF + base_col + HALF)
+            ref[index, :, cols] += jnp.where(codes == leaf, terms, 0.0)
+
+    class Slot:
+        def __init__(self, k, slot_index):
+            step = STAGES[k]
+            i = lax.rem(x + step, RING)
+            first = RING + x - i - 1
+            other = jnp.where(i < x, x - i - 1, 2 * RING + x - i - 1)
+            if step == 0:
+                second_half, half_a, half_b, up_a, up_b = slot_index >= SLOTS, other, first, 2, 1
+            else:
+                second_half, half_a, half_b = slot_index >= SLOTS, first, other
+                up_a, up_b = 1, jnp.where(i < x, 0, 2)
+            offset = jnp.where(second_half, half_b, half_a)
+            at = slot_index - jnp.where(second_half, SLOTS, 0)
+            lows, highs = (low_s, high_s) if step == 0 else (codes_s.at[k - 1, 0], codes_s.at[k - 1, 1])
+            self.low, self.high = lows[offset, at], highs[offset, at]
+            self.which = jnp.where(second_half, up_b, up_a)
+            self.bank = k % 2
+            self.k = k
+
+        def rows(self, at):
+            return lower[self.bank, jnp.maximum(self.low, 0), at : at + HALF, :], upper[self.which, self.high]
+
+        def left(self):
+            return upper_vectors[self.which, self.high], lower_vectors[self.bank, jnp.maximum(self.low, 0)]
+
+        def add_low(self, base_col, terms):
+            masked(acc_low, self.k, self.low, base_col, terms)
+
+        def add_high(self, base_col, terms):
+            masked(acc_up, self.which, jnp.where(self.low >= 0, self.high, -1), base_col, terms)
+
+    class Own:
+        def __init__(self, low, high):
+            self.low, self.high = low, high
+
+        def rows(self, at):
+            return lower[0, self.low, at : at + HALF, :], upper[0, self.high]
+
+        def left(self):
+            return upper_vectors[0, self.high], upper_vectors[0, self.low]
+
+        def add_low(self, base_col, terms):
+            at = self.low * LEAF + base_col
+            acc_low[0, :, at : at + HALF] += terms
+
+        def add_high(self, base_col, terms):
+            at = self.high * LEAF + base_col
+            acc_up[0, :, at : at + HALF] += terms
+
+    def make(item, out_ref):
+        for at in (0, HALF):
+            tile_rows(*item.rows(at), out_ref, at)
+
+    def step_pair(made, made_ref, used, used_ref, both_ways=True):
+        high_values, low_values = used.left()
+        if both_ways:
+            used.add_low(0, nt(high_values, used_ref[0:HALF, :]))
+        if made is not None:
+            tile_rows(*made.rows(0), made_ref, 0)
+        if both_ways:
+            used.add_low(HALF, nt(high_values, used_ref[HALF:LEAF, :]))
+        used.add_high(0, nn(low_values, used_ref[:, 0:HALF]))
+        if made is not None:
+            tile_rows(*made.rows(HALF), made_ref, HALF)
+        used.add_high(HALF, nn(low_values, used_ref[:, HALF:LEAF]))
+
+    tiles = (tile_a, tile_b)
+
+    def run(items, after):
+        for n, item in enumerate(items):
+            made = items[n + 1] if n + 1 < len(items) else after
+            step_pair(made, tiles[(n + 1) % 2], item, tiles[n % 2])
+
+    def stage_loop(k, first, count):
+        width = 2 * UNROLL
+
+        def trip(m, carry):
+            at = first + m * width
+            run([Slot(k, at + n) for n in range(width)], Slot(k, at + width))
+            return carry
+
+        lax.fori_loop(0, count // width, trip, 0)
+
+    def stage_rest(k, first, count, after):
+        run([Slot(k, first + n) for n in range(count)], after)
+
+    def give_back(slot, terms, device):
+        send_terms[slot] = terms.astype(BF)
+        return send(send_terms.at[slot], got_terms.at[slot], back_send.at[slot], back_recv.at[slot], device)
+
+    def land(*slots):
+        for slot in slots:
+            for copy in near[slot]:
+                copy.wait_recv()
+
+    def land_lower(k, slot):
+        build_lower(got_points.at[slot], lower.at[k % 2])
+        build_leaves(got_vectors.at[slot], lower_vectors.at[k % 2])
+
+    own_pairs = [Own(a, b) for a in range(LPD) for b in range(a + 1, LPD)]
+    make(own_pairs[0], tile_a)
+    run(own_pairs[:4], own_pairs[4])
+    land(1)
+    build_upper(got_points.at[1], upper, 2)
+    build_leaves(got_vectors.at[1], upper_vectors.at[2])
+    run(own_pairs[4:], Slot(0, 0))
+
+    width = 2 * UNROLL
+    stage_loop(0, 0, SLOTS - width)
+    land(0)
     build_upper(got_points.at[0], upper, 1)
-    build_upper(got_points.at[1], upper, 2)
     build_leaves(got_vectors.at[0], upper_vectors.at[1])
-    build_leaves(got_vectors.at[1], upper_vectors.at[2])
-
-    def stage(k, step, low_codes, high_codes):
-        i = lax.rem(x + step, RING)
-        first = RING + x - i - 1
-        other = jnp.where(i < x, x - i - 1, 2 * RING + x - i - 1)
-        other_upper = jnp.where(i < x, 0, 2)
-
-        def slot(n):
-            far_half = n >= SLOTS
-            offset = jnp.where(far_half, other, first)
-            which = jnp.where(far_half, other_upper, 1)
-            at = n - jnp.where(far_half, SLOTS, 0)
-            return low_codes[offset, at], high_codes[offset, at], which
-
-        def make(n, tile_ref):
-            low, high, which = slot(n)
-            kernel_tile(lower, upper, which, jnp.maximum(low, 0), high, tile_ref)
-
-        def apply(n, tile_ref):
-            low, high, which = slot(n)
-            tile = tile_ref[...]
-            to_upper = nn(lower_vectors[jnp.maximum(low, 0)], tile)
-            to_lower = nt(upper_vectors[which, high], tile)
-            live = low >= 0
-            for leaf in range(LPD):
-                cols = slice(leaf * LEAF, (leaf + 1) * LEAF)
-                acc_up[which, :, cols] += jnp.where(live & (high == leaf), to_upper, 0.0)
-                acc_low[k, :, cols] += jnp.where(low == leaf, to_lower, 0.0)
-
-        make(0, tile_a)
-
-        def pair(m, carry):
-            make(2 * m + 1, tile_b)
-            apply(2 * m, tile_a)
-            make(jnp.minimum(2 * m + 2, 2 * SLOTS - 1), tile_a)
-            apply(2 * m + 1, tile_b)
-            return carry
-
-        lax.fori_loop(0, SLOTS, pair, 0)
-
-    stage(0, 0, low_s, high_s)
-
+    stage_loop(0, SLOTS - width, SLOTS)
+
+    land(2, 3)
+    forwards = []
+    for part_index, (slot, step, start) in enumerate(((2, 3, 0), (3, 1, half))):
+        cols = pl.ds(start, half)
+        to = in_ring(step)
+        for which, ref in enumerate((got_points, got_vectors)):
+            sem = 2 * part_index + which
+            forwards.append(
+                send(ref.at[slot, :, cols], ref.at[4, :, cols], pass_send.at[sem], pass_recv.at[sem], to)
+            )
     for copy in share_copies:
         copy.wait_recv()
-    mine = pl.ds(pl.multiple_of(gy * CHUNK, CHUNK), CHUNK)
     total = share[mine, :]
     for s in range(NGY - 1):
         total += share_got[s]
     chunk_sum[...] = total
     roots[0] = total
     targets[mine, :] = total
-
-    for slot in (2, 3):
-        for copy in near[slot]:
-            copy.wait_recv()
-    half = BLOCK // 2
-    forwards = []
-    for part_index, (slot, step, start) in enumerate(((2, 3, 0), (3, 1, half))):
-        cols = pl.ds(start, half)
-        to = in_ring(step)
-        forwards.append(
-            send(
-                got_points.at[slot, :, cols],
-                got_points.at[4, :, cols],
-                pass_send.at[2 * part_index],
-                pass_recv.at[2 * part_index],
-                to,
-            )
-        )
-        forwards.append(
-            send(
-                got_vectors.at[slot, :, cols],
-                got_vectors.at[4, :, cols],
-                pass_send.at[2 * part_index + 1],
-                pass_recv.at[2 * part_index + 1],
-                to,
-            )
-        )
-    root_copies = []
-    for s in range(1, NGX):
-        root_copies.append(
-            send(chunk_sum, roots.at[NGX - s], root_send.at[s - 1], root_recv.at[s - 1], mate_gx(s))
-        )
-    target_copies = []
-    for s in range(1, NGY):
-        target_copies.append(
-            send(chunk_sum, targets.at[mine, :], target_send.at[s - 1], target_recv.at[s - 1], mate_gy(s))
-        )
     for pair in code_copies:
         for copy in pair:
             copy.wait_recv()
@@ -392,34 +409,34 @@
             local.append(copy)
     for copy in local:
         copy.wait()
-
-    def give_back(slot, terms, device):
-        send_terms[slot] = terms.astype(BF)
-        return send(send_terms.at[slot], got_terms.at[slot], back_send.at[slot], back_recv.at[slot], device)
-
-    returned = []
-
-    def ring_stage(k, step, slot):
-        build_lower(got_points.at[slot], lower)
-        build_leaves(got_vectors.at[slot], lower_vectors)
-        stage(
-            k,
-            step,
-            codes_s.at[slot - 2, 0],
-            codes_s.at[slot - 2, 1],
-        )
-
-    ring_stage(1, 1, 2)
-    returned.append(give_back(2, acc_low[1], in_ring(1)))
+    land_lower(1, 2)
+    stage_rest(0, 2 * SLOTS - width, width, Slot(1, 0))
+
+    root_copies = []
+    for s in range(1, NGX):
+        root_copies.append(
+            send(chunk_sum, roots.at[NGX - s], root_send.at[s - 1], root_recv.at[s - 1], mate_gx(s))
+        )
+    target_copies = []
+    for s in range(1, NGY):
+        target_copies.append(
+            send(chunk_sum, targets.at[mine, :], target_send.at[s - 1], target_recv.at[s - 1], mate_gy(s))
+        )
+
+    stage_loop(1, 0, 2 * SLOTS - width)
+    for copy in forwards:
+        copy.wait_recv()
+    land_lower(2, 4)
+    stage_rest(1, 2 * SLOTS - width, width, Slot(2, 0))
+    returned = [give_back(2, acc_low[1], in_ring(1))]
 
     for copy in root_copies:
         copy.wait_recv()
     for copy in target_copies:
         copy.wait_recv()
     sources = roots[...].reshape(NGX * CHUNK, SKEL)
-    goals = targets[...]
     source_points = sources[:, 0:DIM]
-    goal_points = goals.T[0:DIM, :]
+    goal_points = targets[...].T[0:DIM, :]
     source_norm = jnp.sum(source_points * source_points, axis=1, keepdims=True)
     goal_norm = jnp.sum(goal_points * goal_points, axis=0, keepdims=True)
     products = nn(source_points.astype(BF), goal_points.astype(BF))
@@ -430,20 +447,27 @@
     flags = jnp.sum(jnp.where(listed, far_mask_ref[...].astype(F32), 0.0), axis=1, keepdims=True)
     flagged = (sources * flags).T[DIM : DIM + COLS, :]
     part[...] = nn(flagged, root_kernel, lax.Precision.HIGHEST)
+
+    stage_loop(2, 0, 2 * SLOTS - width)
     part_copies = []
     for s in range(1, NGY):
         part_copies.append(
             send(part, part_got.at[s - 1], part_send.at[s - 1], part_recv.at[s - 1], mate_gy(s))
         )
-
-    ring_stage(2, 3, 3)
-    returned.append(give_back(3, acc_low[2], in_ring(3)))
-    for copy in forwards:
-        copy.wait_recv()
-    ring_stage(3, 2, 4)
-    returned.append(give_back(4, acc_low[3], in_ring(2)))
+    land_lower(3, 3)
+    stage_rest(2, 2 * SLOTS - width, width, Slot(3, 0))
+    returned.append(give_back(4, acc_low[2], in_ring(2)))
+
+    stage_loop(3, 0, 2 * SLOTS - width)
     returned.append(give_back(0, acc_up[1], at_flat(4)))
+    diagonal = [Own(leaf, leaf) for leaf in range(LPD)]
+    build_lower(points_ref, lower.at[0])
+    stage_rest(3, 2 * SLOTS - width, width, diagonal[0])
+    returned.append(give_back(3, acc_low[3], in_ring(3)))
     returned.append(give_back(1, acc_up[2], at_flat(8)))
+    for n in range(LPD):
+        made = diagonal[n + 1] if n + 1 < LPD else None
+        step_pair(made, tiles[(n + 1) % 2], diagonal[n], tiles[n % 2], both_ways=False)
 
     for copy in part_copies:
         copy.wait_recv()
@@ -489,16 +513,18 @@
     return pl.pallas_call(
         fused,
         out_shape=jax.ShapeDtypeStruct((COLS, BLOCK), F32),
-        in_specs=[vmem] * 9 + [smem] * 2 + [vmem] * 2,
+        in_specs=[pl.BlockSpec(memory_space=pltpu.HBM)] * 2 + [vmem] * 7 + [smem] * 2 + [vmem] * 2,
         out_specs=vmem,
         scratch_shapes=[
+            pltpu.VMEM((DIM, BLOCK), BF),
+            pltpu.VMEM((COLS, BLOCK), BF),
             pltpu.VMEM((5, DIM, BLOCK), BF),
             pltpu.VMEM((5, COLS, BLOCK), BF),
             pltpu.VMEM((3, LPD, COLS, LEAF), BF),
-            pltpu.VMEM((LPD, COLS, LEAF), BF),
+            pltpu.VMEM((2, LPD, COLS, LEAF), BF),
             pltpu.VMEM((3, 2, reach, SLOTS), jnp.int32),
             pltpu.SMEM((3, 2, reach, SLOTS), jnp.int32),
-            pltpu.VMEM((LPD, LEAF, AUG), BF),
+            pltpu.VMEM((2, LPD, LEAF, AUG), BF),
             pltpu.VMEM((3, LPD, AUG, LEAF), BF),
             pltpu.VMEM((RING, COLS, BLOCK), F32),
             pltpu.VMEM((3, COLS, BLOCK), F32),
@@ -519,6 +545,7 @@
             dma((6,)),
             dma((6,)),
             dma((6,)),
+            dma((2,)),
             dma((4,)),
             dma((4,)),
             dma((5,)),

time: 79.9 us -> 63.6 us (0.80)
  Pallas kernels: 78.1 us -> 61.7 us
    pallas_call x1, Pallas kernels: 78.1 us -> 61.7 us  [on_device(): pl.pallas_call(fused, out_shape=jax.ShapeDtypeStruct((COLS, BLOCK), F32),...]
where the time goes in v1:
time: 63.6 us; the launch traced here: 63.4 us
  Pallas kernels  61.7 us (97%)
  local copies, waits for them, and re-layouts  1.67 us (3%)
    pallas_call x1, Pallas kernels, on_device(): pl.pallas_call(fused, out_shape=jax.ShapeDtypeStruct((COLS, BLOCK), F32),...  61.7 us
    unnamed x1, local copies, waits for them, and re-layouts  1.67 us

profile of v1, /device:TPU:0, one launch (start us, length us, event | category | flops | bytes accessed | tf_op | source)
XLA Modules:
  0.0 63.4 jit_solution(6446650455529661112)
XLA Ops:
  0.0 61.7 %treecode.1 = f32[32,2048]{1,0:T(8,128)} custom-call(bf16[64,2048]{1,0:T(8,128)(2,1)} %points_hbm.1, bf16[32,2048]{1,0:T(8,128)(2,1)} %vectors_hbm.1, s32[4,128]{1,0:T(4,128)} %leaf_pick_ref.1, s32[4,512]{1,0:T(4,128)} %leaf_assign_ref.1, s32[1,128]{1,0:T(1,128)} %device_pick_ref.1, s32[1,512]{1,0:T(1,128)} %device_assign_ref.1, s32[7,1,128]{2,1,0:T(1,128)} %bitcast.9, ...), custom_call_target="tpu_custom_call" | custom-call | tf_op jit(solution)/shard_map/treecode/pallas_call | solution.py:513
  61.8 1.7 %copy.13 = f32[32,2048]{1,0:T(8,128)} copy(f32[32,2048]{1,0:T(8,128)} %treecode.1) | data formatting | bytes 524288

commit v2 on v1

--- a/solution.py
+++ b/solution.py
@@ -17,7 +17,6 @@
 RING = 4
 AUG = 128
 CHUNK = SKEL // NGY
-STAGES = (0, 1, 2, 3)
 HALF = LEAF // 2
 UNROLL = 3
 MESH = pl.DeviceIdType.MESH
@@ -89,8 +88,6 @@
     node_pick_ref,
     node_assign_ref,
     far_mask_ref,
-    low_s,
-    high_s,
     low_v,
     high_v,
     out_ref,
@@ -142,6 +139,8 @@
     flat = gx * NGY + gy
     x = gy % RING
     base = gy - x
+    near_step = 1 + 2 * (gx % 2)
+    steps = (0, near_step, RING - near_step, 2)
 
     def at_flat(step):
         other = lax.rem(flat + step + NGX * NGY, NGX * NGY)
@@ -164,6 +163,8 @@
     own_copies = [
         pltpu.make_async_copy(points_hbm, points_ref, own_sem.at[0]),
         pltpu.make_async_copy(vectors_hbm, vectors_ref, own_sem.at[1]),
+        pltpu.make_async_copy(low_v, codes_s.at[0, 0], code_local.at[6]),
+        pltpu.make_async_copy(high_v, codes_s.at[0, 1], code_local.at[7]),
     ]
     for copy in own_copies:
         copy.start()
@@ -193,7 +194,7 @@
         return copy
 
     code_copies = []
-    for k, step in enumerate(STAGES[1:]):
+    for k, step in enumerate(steps[1:]):
         to = in_ring(RING - step)
         code_copies.append(
             (
@@ -211,9 +212,7 @@
         )
 
     send_block(1, at_flat(-8))
-    send_block(0, at_flat(-4))
-    send_block(2, in_ring(3))
-    send_block(3, in_ring(1))
+    send_block(2, in_ring(RING - near_step))
 
     heaps = (3 + gy // 2, 1 + gy // 4, 0)
     sides = (gy % 2, (gy // 2) % 2, gy // 4)
@@ -267,29 +266,20 @@
             ref[index, :, cols] += jnp.where(codes == leaf, terms, 0.0)
 
     class Slot:
-        def __init__(self, k, slot_index):
-            step = STAGES[k]
+        def __init__(self, k, step, first_half, at):
             i = lax.rem(x + step, RING)
             first = RING + x - i - 1
             other = jnp.where(i < x, x - i - 1, 2 * RING + x - i - 1)
-            if step == 0:
-                second_half, half_a, half_b, up_a, up_b = slot_index >= SLOTS, other, first, 2, 1
-            else:
-                second_half, half_a, half_b = slot_index >= SLOTS, first, other
-                up_a, up_b = 1, jnp.where(i < x, 0, 2)
-            offset = jnp.where(second_half, half_b, half_a)
-            at = slot_index - jnp.where(second_half, SLOTS, 0)
-            lows, highs = (low_s, high_s) if step == 0 else (codes_s.at[k - 1, 0], codes_s.at[k - 1, 1])
-            self.low, self.high = lows[offset, at], highs[offset, at]
-            self.which = jnp.where(second_half, up_b, up_a)
-            self.bank = k % 2
+            offset = jnp.where(first_half, first, other)
+            self.low, self.high = codes_s[k, 0, offset, at], codes_s[k, 1, offset, at]
+            self.which = jnp.where(first_half, 1, jnp.where(i < x, 0, 2))
             self.k = k
 
         def rows(self, at):
-            return lower[self.bank, jnp.maximum(self.low, 0), at : at + HALF, :], upper[self.which, self.high]
+            return lower[self.k, jnp.maximum(self.low, 0), at : at + HALF, :], upper[self.which, self.high]
 
         def left(self):
-            return upper_vectors[self.which, self.high], lower_vectors[self.bank, jnp.maximum(self.low, 0)]
+            return upper_vectors[self.which, self.high], lower_vectors[self.k, jnp.maximum(self.low, 0)]
 
         def add_low(self, base_col, terms):
             masked(acc_low, self.k, self.low, base_col, terms)
@@ -339,18 +329,18 @@
             made = items[n + 1] if n + 1 < len(items) else after
             step_pair(made, tiles[(n + 1) % 2], item, tiles[n % 2])
 
-    def stage_loop(k, first, count):
-        width = 2 * UNROLL
-
+    width = 2 * UNROLL
+
+    def stage_loop(slot, count):
         def trip(m, carry):
-            at = first + m * width
-            run([Slot(k, at + n) for n in range(width)], Slot(k, at + width))
+            at = m * width
+            run([slot(at + n) for n in range(width)], slot(at + width))
             return carry
 
         lax.fori_loop(0, count // width, trip, 0)
 
-    def stage_rest(k, first, count, after):
-        run([Slot(k, first + n) for n in range(count)], after)
+    def stage_rest(slot, first, after):
+        run([slot(first + n) for n in range(width)], after)
 
     def give_back(slot, terms, device):
         send_terms[slot] = terms.astype(BF)
@@ -362,34 +352,61 @@
                 copy.wait_recv()
 
     def land_lower(k, slot):
-        build_lower(got_points.at[slot], lower.at[k % 2])
-        build_leaves(got_vectors.at[slot], lower_vectors.at[k % 2])
+        land(slot)
+        build_lower(got_points.at[slot], lower.at[k])
+        build_leaves(got_vectors.at[slot], lower_vectors.at[k])
+
+    def other_of(k):
+        return lambda n: Slot(k, steps[k], False, n)
+
+    def first_of_three(n):
+        k = n // SLOTS
+        step = jnp.where(k == 0, 0, jnp.where(k == 1, steps[1], steps[2]))
+        return Slot(k, step, True, n - k * SLOTS)
+
+    def last_two(n):
+        first_half = n < SLOTS
+        return Slot(3, steps[3], first_half, n - jnp.where(first_half, 0, SLOTS))
 
     own_pairs = [Own(a, b) for a in range(LPD) for b in range(a + 1, LPD)]
     make(own_pairs[0], tile_a)
     run(own_pairs[:4], own_pairs[4])
+    for copy in near[2]:
+        copy.wait_send()
+    send_block(3, in_ring(near_step))
+    send_block(0, at_flat(-4))
     land(1)
     build_upper(got_points.at[1], upper, 2)
     build_leaves(got_vectors.at[1], upper_vectors.at[2])
-    run(own_pairs[4:], Slot(0, 0))
-
-    width = 2 * UNROLL
-    stage_loop(0, 0, SLOTS - width)
-    land(0)
-    build_upper(got_points.at[0], upper, 1)
-    build_leaves(got_vectors.at[0], upper_vectors.at[1])
-    stage_loop(0, SLOTS - width, SLOTS)
-
-    land(2, 3)
+    run(own_pairs[4:], other_of(0)(0))
+
+    stage_loop(other_of(0), width)
+    for pair in code_copies:
+        for copy in pair:
+            copy.wait_recv()
+    local = []
+    for k in range(3):
+        for h in range(2):
+            copy = pltpu.make_async_copy(codes_v.at[k, h], codes_s.at[k + 1, h], code_local.at[2 * k + h])
+            copy.start()
+            local.append(copy)
+    for copy in local:
+        copy.wait()
+    land_lower(1, 2)
+    stage_rest(other_of(0), width, other_of(1)(0))
+
+    stage_loop(other_of(1), width)
+    land_lower(2, 3)
     forwards = []
-    for part_index, (slot, step, start) in enumerate(((2, 3, 0), (3, 1, half))):
-        cols = pl.ds(start, half)
-        to = in_ring(step)
+    for part_index, slot in enumerate((2, 3)):
+        cols = pl.ds(part_index * half, half)
+        to = in_ring(RING - steps[1 + part_index])
         for which, ref in enumerate((got_points, got_vectors)):
             sem = 2 * part_index + which
             forwards.append(
                 send(ref.at[slot, :, cols], ref.at[4, :, cols], pass_send.at[sem], pass_recv.at[sem], to)
             )
+    near[4] = forwards
     for copy in share_copies:
         copy.wait_recv()
     total = share[mine, :]
@@ -398,19 +415,7 @@
     chunk_sum[...] = total
     roots[0] = total
     targets[mine, :] = total
-    for pair in code_copies:
-        for copy in pair:
-            copy.wait_recv()
-    local = []
-    for k in range(3):
-        for h in range(2):
-            copy = pltpu.make_async_copy(codes_v.at[k, h], codes_s.at[k, h], code_local.at[2 * k + h])
-            copy.start()
-            local.append(copy)
-    for copy in local:
-        copy.wait()
-    land_lower(1, 2)
-    stage_rest(0, 2 * SLOTS - width, width, Slot(1, 0))
+    stage_rest(other_of(1), width, other_of(2)(0))
 
     root_copies = []
     for s in range(1, NGX):
@@ -422,14 +427,14 @@
         target_copies.append(
             send(chunk_sum, targets.at[mine, :], target_send.at[s - 1], target_recv.at[s - 1], mate_gy(s))
         )
-
-    stage_loop(1, 0, 2 * SLOTS - width)
-    for copy in forwards:
-        copy.wait_recv()
-    land_lower(2, 4)
-    stage_rest(1, 2 * SLOTS - width, width, Slot(2, 0))
-    returned = [give_back(2, acc_low[1], in_ring(1))]
-
+    stage_loop(other_of(2), width)
+    land(0)
+    build_upper(got_points.at[0], upper, 1)
+    build_leaves(got_vectors.at[0], upper_vectors.at[1])
+    stage_rest(other_of(2), width, first_of_three(0))
+
+    stage_loop(first_of_three, 3 * SLOTS - width)
+    land_lower(3, 4)
     for copy in root_copies:
         copy.wait_recv()
     for copy in target_copies:
@@ -447,23 +452,19 @@
     flags = jnp.sum(jnp.where(listed, far_mask_ref[...].astype(F32), 0.0), axis=1, keepdims=True)
     flagged = (sources * flags).T[DIM : DIM + COLS, :]
     part[...] = nn(flagged, root_kernel, lax.Precision.HIGHEST)
-
-    stage_loop(2, 0, 2 * SLOTS - width)
+    stage_rest(first_of_three, 3 * SLOTS - width, last_two(0))
     part_copies = []
     for s in range(1, NGY):
         part_copies.append(
             send(part, part_got.at[s - 1], part_send.at[s - 1], part_recv.at[s - 1], mate_gy(s))
         )
-    land_lower(3, 3)
-    stage_rest(2, 2 * SLOTS - width, width, Slot(3, 0))
-    returned.append(give_back(4, acc_low[2], in_ring(2)))
-
-    stage_loop(3, 0, 2 * SLOTS - width)
+    returned = [give_back(2, acc_low[1], in_ring(steps[1])), give_back(3, acc_low[2], in_ring(steps[2]))]
+
+    stage_loop(last_two, 2 * SLOTS - width)
     returned.append(give_back(0, acc_up[1], at_flat(4)))
     diagonal = [Own(leaf, leaf) for leaf in range(LPD)]
-    build_lower(points_ref, lower.at[0])
-    stage_rest(3, 2 * SLOTS - width, width, diagonal[0])
-    returned.append(give_back(3, acc_low[3], in_ring(3)))
+    stage_rest(last_two, 2 * SLOTS - width, diagonal[0])
+    returned.append(give_back(4, acc_low[3], in_ring(2)))
     returned.append(give_back(1, acc_up[2], at_flat(8)))
     for n in range(LPD):
         made = diagonal[n + 1] if n + 1 < LPD else None
@@ -489,7 +490,8 @@
         total_terms += got_terms[slot].astype(F32)
     out_ref[...] = total_terms
     for copy in started:
-        copy.wait_send()
+        if not any(copy is done for done in near[2]):
+            copy.wait_send()
 
 
 def on_device(
@@ -506,14 +508,13 @@
     near_upper,
 ):
     vmem = pl.BlockSpec(memory_space=pltpu.VMEM)
-    smem = pl.BlockSpec(memory_space=pltpu.SMEM)
     dma = pltpu.SemaphoreType.DMA
     low, high = near_lower[0], near_upper[0]
     reach = low.shape[0]
     return pl.pallas_call(
         fused,
         out_shape=jax.ShapeDtypeStruct((COLS, BLOCK), F32),
-        in_specs=[pl.BlockSpec(memory_space=pltpu.HBM)] * 2 + [vmem] * 7 + [smem] * 2 + [vmem] * 2,
+        in_specs=[pl.BlockSpec(memory_space=pltpu.HBM)] * 2 + [vmem] * 9,
         out_specs=vmem,
         scratch_shapes=[
             pltpu.VMEM((DIM, BLOCK), BF),
@@ -521,10 +522,10 @@
             pltpu.VMEM((5, DIM, BLOCK), BF),
             pltpu.VMEM((5, COLS, BLOCK), BF),
             pltpu.VMEM((3, LPD, COLS, LEAF), BF),
-            pltpu.VMEM((2, LPD, COLS, LEAF), BF),
+            pltpu.VMEM((RING, LPD, COLS, LEAF), BF),
             pltpu.VMEM((3, 2, reach, SLOTS), jnp.int32),
-            pltpu.SMEM((3, 2, reach, SLOTS), jnp.int32),
-            pltpu.VMEM((2, LPD, LEAF, AUG), BF),
+            pltpu.SMEM((RING, 2, reach, SLOTS), jnp.int32),
+            pltpu.VMEM((RING, LPD, LEAF, AUG), BF),
             pltpu.VMEM((3, LPD, AUG, LEAF), BF),
             pltpu.VMEM((RING, COLS, BLOCK), F32),
             pltpu.VMEM((3, COLS, BLOCK), F32),
@@ -544,7 +545,7 @@
             dma((10,)),
             dma((6,)),
             dma((6,)),
-            dma((6,)),
+            dma((8,)),
             dma((2,)),
             dma((4,)),
             dma((4,)),
@@ -575,8 +576,6 @@
         far_mask,
         low,
         high,
-        low,
-        high,
     )
 
 

time: 63.6 us -> 58.5 us (0.920)
  Pallas kernels: 61.7 us -> 56.7 us
    pallas_call x1, Pallas kernels: 61.7 us -> 56.7 us  [on_device(): pl.pallas_call(fused, out_shape=jax.ShapeDtypeStruct((COLS, BLOCK), F32),...]
where the time goes in v2:
time: 58.5 us; the launch traced here: 58.3 us
  Pallas kernels  56.7 us (97%)
  local copies, waits for them, and re-layouts  1.67 us (3%)
    pallas_call x1, Pallas kernels, on_device(): pl.pallas_call(fused, out_shape=jax.ShapeDtypeStruct((COLS, BLOCK), F32),...  56.7 us
    unnamed x1, local copies, waits for them, and re-layouts  1.67 us

profile of v2, /device:TPU:0, one launch (start us, length us, event | category | flops | bytes accessed | tf_op | source)
XLA Modules:
  0.0 58.3 jit_solution(11742367486290314468)
XLA Ops:
  0.0 56.7 %treecode.1 = f32[32,2048]{1,0:T(8,128)} custom-call(bf16[64,2048]{1,0:T(8,128)(2,1)} %points_hbm.1, bf16[32,2048]{1,0:T(8,128)(2,1)} %vectors_hbm.1, s32[4,128]{1,0:T(4,128)} %leaf_pick_ref.1, s32[4,512]{1,0:T(4,128)} %leaf_assign_ref.1, s32[1,128]{1,0:T(1,128)} %device_pick_ref.1, s32[1,512]{1,0:T(1,128)} %device_assign_ref.1, s32[7,1,128]{2,1,0:T(1,128)} %bitcast.7, ...), custom_call_target="tpu_custom_call" | custom-call | tf_op jit(solution)/shard_map/treecode/pallas_call | solution.py:514
  56.7 1.7 %copy.13 = f32[32,2048]{1,0:T(8,128)} copy(f32[32,2048]{1,0:T(8,128)} %treecode.1) | data formatting | bytes 524288

commit v3 on v2

--- a/solution.py
+++ b/solution.py
@@ -324,8 +324,10 @@
 
     tiles = (tile_a, tile_b)
 
-    def run(items, after):
+    def run(items, after, before_last=None):
         for n, item in enumerate(items):
+            if before_last is not None and n + 1 == len(items):
+                before_last()
             made = items[n + 1] if n + 1 < len(items) else after
             step_pair(made, tiles[(n + 1) % 2], item, tiles[n % 2])
 
@@ -339,8 +341,8 @@
 
         lax.fori_loop(0, count // width, trip, 0)
 
-    def stage_rest(slot, first, after):
-        run([slot(first + n) for n in range(width)], after)
+    def stage_rest(slot, first, after, before_last=None):
+        run([slot(first + n) for n in range(width)], after, before_last)
 
     def give_back(slot, terms, device):
         send_terms[slot] = terms.astype(BF)
@@ -375,10 +377,13 @@
         copy.wait_send()
     send_block(3, in_ring(near_step))
     send_block(0, at_flat(-4))
-    land(1)
-    build_upper(got_points.at[1], upper, 2)
-    build_leaves(got_vectors.at[1], upper_vectors.at[2])
-    run(own_pairs[4:], other_of(0)(0))
+
+    def land_upper(slot, which):
+        land(slot)
+        build_upper(got_points.at[slot], upper, which)
+        build_leaves(got_vectors.at[slot], upper_vectors.at[which])
+
+    run(own_pairs[4:], other_of(0)(0), lambda: land_upper(1, 2))
 
     stage_loop(other_of(0), width)
     for pair in code_copies:
@@ -415,7 +420,7 @@
     chunk_sum[...] = total
     roots[0] = total
     targets[mine, :] = total
-    stage_rest(other_of(1), width, other_of(2)(0))
+    stage_rest(other_of(1), width, first_of_three(0), lambda: land_upper(0, 1))
 
     root_copies = []
     for s in range(1, NGX):
@@ -427,11 +432,6 @@
         target_copies.append(
             send(chunk_sum, targets.at[mine, :], target_send.at[s - 1], target_recv.at[s - 1], mate_gy(s))
         )
-    stage_loop(other_of(2), width)
-    land(0)
-    build_upper(got_points.at[0], upper, 1)
-    build_leaves(got_vectors.at[0], upper_vectors.at[1])
-    stage_rest(other_of(2), width, first_of_three(0))
 
     stage_loop(first_of_three, 3 * SLOTS - width)
     land_lower(3, 4)
@@ -458,13 +458,16 @@
         part_copies.append(
             send(part, part_got.at[s - 1], part_send.at[s - 1], part_recv.at[s - 1], mate_gy(s))
         )
-    returned = [give_back(2, acc_low[1], in_ring(steps[1])), give_back(3, acc_low[2], in_ring(steps[2]))]
+    returned = [give_back(2, acc_low[1], in_ring(steps[1]))]
 
     stage_loop(last_two, 2 * SLOTS - width)
     returned.append(give_back(0, acc_up[1], at_flat(4)))
     diagonal = [Own(leaf, leaf) for leaf in range(LPD)]
-    stage_rest(last_two, 2 * SLOTS - width, diagonal[0])
+    stage_rest(last_two, 2 * SLOTS - width, other_of(2)(0))
     returned.append(give_back(4, acc_low[3], in_ring(2)))
+    stage_loop(other_of(2), width)
+    stage_rest(other_of(2), width, diagonal[0])
+    returned.append(give_back(3, acc_low[2], in_ring(steps[2])))
     returned.append(give_back(1, acc_up[2], at_flat(8)))
     for n in range(LPD):
         made = diagonal[n + 1] if n + 1 < LPD else None

time: 58.5 us -> 58.2 us (level); the launches traced: 58.3 us -> 57.4 us
  Pallas kernels: 56.7 us -> 55.7 us
    pallas_call x1, Pallas kernels: 56.7 us -> 55.7 us  [on_device(): pl.pallas_call(fused, out_shape=jax.ShapeDtypeStruct((COLS, BLOCK), F32),...]
where the time goes in v3:
time: 58.2 us; the launch traced here: 57.4 us
  Pallas kernels  55.7 us (96%)
  local copies, waits for them, and re-layouts  1.67 us (3%)
    pallas_call x1, Pallas kernels, on_device(): pl.pallas_call(fused, out_shape=jax.ShapeDtypeStruct((COLS, BLOCK), F32),...  55.7 us
    unnamed x1, local copies, waits for them, and re-layouts  1.67 us

profile of v3, /device:TPU:0, one launch (start us, length us, event | category | flops | bytes accessed | tf_op | source)
XLA Modules:
  0.0 57.4 jit_solution(5954123407476647944)
XLA Ops:
  0.0 55.7 %treecode.1 = f32[32,2048]{1,0:T(8,128)} custom-call(bf16[64,2048]{1,0:T(8,128)(2,1)} %points_hbm.1, bf16[32,2048]{1,0:T(8,128)(2,1)} %vectors_hbm.1, s32[4,128]{1,0:T(4,128)} %leaf_pick_ref.1, s32[4,512]{1,0:T(4,128)} %leaf_assign_ref.1, s32[1,128]{1,0:T(1,128)} %device_pick_ref.1, s32[1,512]{1,0:T(1,128)} %device_assign_ref.1, s32[7,1,128]{2,1,0:T(1,128)} %bitcast.7, ...), custom_call_target="tpu_custom_call" | custom-call | tf_op jit(solution)/shard_map/treecode/pallas_call | solution.py:517
  55.7 1.7 %copy.13 = f32[32,2048]{1,0:T(8,128)} copy(f32[32,2048]{1,0:T(8,128)} %treecode.1) | data formatting | bytes 524288
